TPU v7x, 512 devices: a whole 4x8x8 slice. The times are simulated.
512 devices in a mesh: band: 16 (over y, core), aperture: 32 (over x, z).
Axes of the slice: x: 4, y: 8, z: 8, core: 2. Of those that a mesh axis runs over, the one named last changes fastest.
Arguments:
- raw_echoes: bfloat16 [16384, 2, 4096], P('aperture', None, 'band'), may hold values from -6 to 6
- pulse_order: int32 [32, 16, 32], P('aperture', 'band'), may hold values from 0 to 31, each once within a row
- matched: float32 [2, 4096], replicated, may hold values from -6 to 6
- offsets: int32 [14, 2, 2, 1], replicated, may hold values from 0 to 16
- fraction: float32 [14, 2, 2], replicated, may hold values from 0 to 0.4
- tilt_angle: float32 [14, 2], replicated, may hold values from -3.140625 to 3.140625
Outputs:
- speckle_image: float32 [16384, 128], P(('band', 'aperture'))
Inputs may be any that keep to these rules, and one draw needn't show every extreme that they name: `pulse_order`: each row of 32 entries names every number below 32 once.
All inputs are finite; a program needn't handle non-finite values.
Results may differ from a plain program's by a relative error of at most 0.0025.
Values may be sent and summed in bfloat16 or wider, within the bound.
A program may use at most 64 MiB of HBM per device.

v0:
```python
import math

import jax
import jax.numpy as jnp
import numpy as np
from jax import lax
from jax.sharding import PartitionSpec as P

FREQ = 4096
R = 128
SHIFT = 8


HIGHEST = lax.Precision.HIGHEST


def swapped(value, axis, apart):
    mask = 2**apart
    pairs = [(source, source ^ mask) for source in range(lax.axis_size(axis))]
    return lax.ppermute(value, axis, pairs)


def split_up(x, dim, peers):
    before, after = (x.shape[:dim], x.shape[dim + 1 :])
    return jnp.moveaxis(x.reshape(*before, peers, -1, *after), dim, 0)


def sent_and_summed(x, axis, dim):
    peers = lax.axis_size(axis)
    pieces = lax.all_to_all(split_up(x, dim, peers), axis, 0, 0, tiled=True)
    return jnp.sum(pieces, axis=0)


def range_table(matched_part, freq_start, bin_count):
    freq_count = matched_part.shape[1]
    freq_index = freq_start + jnp.arange(freq_count, dtype=jnp.int32)
    bin_index = jnp.arange(bin_count, dtype=jnp.int32)
    phase_turns = freq_index[:, None] * bin_index[None, :] % FREQ
    phase_angle = phase_turns.astype(jnp.float32) * (2.0 * math.pi / FREQ)
    cosine = jnp.cos(phase_angle)
    sine_part = jnp.sin(phase_angle)
    spec_real = matched_part[0][:, None]
    spec_imag = matched_part[1][:, None]
    norm_scale = 1.0 / math.sqrt(FREQ)
    table_real = (spec_real * cosine - spec_imag * sine_part) * norm_scale
    table_imag = (spec_real * sine_part + spec_imag * cosine) * norm_scale
    upper_rows = jnp.concatenate([table_real, table_imag], axis=1)
    lower_rows = jnp.concatenate([-table_imag, table_real], axis=1)
    return jnp.concatenate([upper_rows, lower_rows], axis=0).astype(jnp.bfloat16)


def interp_kernel(shift_frac):
    in_pos = jnp.arange(128, dtype=jnp.float32)[:, None]
    out_pos = jnp.arange(128, dtype=jnp.float32)[None, :]
    distance = in_pos - out_pos - shift_frac
    tapered = jnp.sinc(distance) * jnp.exp(-((distance / 2.5) ** 2))
    return jnp.where(jnp.abs(distance) <= 4.0, tapered, jnp.zeros_like(tapered))


def merge_pair(first_child, second_child, tree_level, beam_start, offsets, fraction, tilt_angle):
    sub_count = first_child.shape[0]
    row_count = first_child.shape[1]
    range_width = first_child.shape[3]
    block_count = range_width // 128
    halves = []
    for parity in range(2):
        beam_index = (beam_start + 2 * jnp.arange(row_count, dtype=jnp.int32) + parity).astype(
            jnp.float32
        )
        position = 2.0 * (beam_index + 0.5) / 2.0 ** (tree_level + 1) - 1.0
        summed = jnp.zeros(first_child.shape, jnp.float32)
        for child_index, child_image in enumerate((first_child, second_child)):
            padded = jnp.pad(child_image, ((0, 0), (0, 0), (0, 0), (SHIFT, SHIFT)))
            windows = []
            for block_index in range(block_count):
                start_cell = (
                    block_index * 128 + offsets[tree_level, child_index, parity, block_index]
                ).astype(jnp.int32)
                windows.append(lax.dynamic_slice_in_dim(padded, start_cell, 128, 3))
            stacked = jnp.stack(windows, axis=3)
            kernel = interp_kernel(fraction[tree_level, child_index, parity])
            shifted = jnp.einsum("nrckw,wo->nrcko", stacked, kernel, precision=HIGHEST)
            shifted = shifted.reshape(first_child.shape)
            phase_angle = tilt_angle[tree_level, child_index] * position
            cosine = jnp.cos(phase_angle)[None, :, None]
            sine_part = jnp.sin(phase_angle)[None, :, None]
            real_part = shifted[:, :, 0]
            imag_part = shifted[:, :, 1]
            summed = summed + jnp.stack(
                [
                    real_part * cosine - imag_part * sine_part,
                    real_part * sine_part + imag_part * cosine,
                ],
                axis=2,
            )
        halves.append(summed * (1.0 / math.sqrt(2.0)))
    parent = jnp.stack(halves, axis=2)
    return parent.reshape(sub_count, 2 * row_count, 2, range_width)


def box_sum(values):
    row_count = values.shape[1]
    range_width = values.shape[2]
    padded = jnp.pad(values, ((0, 0), (2, 2), (2, 2)))
    across = padded[:, 0:row_count, :]
    for offset_row in range(1, 5):
        across = across + padded[:, offset_row : offset_row + row_count, :]
    summed = across[:, :, 0:range_width]
    for offset_col in range(1, 5):
        summed = summed + across[:, :, offset_col : offset_col + range_width]
    return summed


def speckle(intensity):
    cell_count = box_sum(jnp.ones(intensity.shape, jnp.float32))
    local_mean = box_sum(intensity) / cell_count
    local_square = box_sum(intensity * intensity) / cell_count
    lee_gain = (local_square - local_mean * local_mean) / (
        local_square - 0.75 * local_mean * local_mean + 0.001
    )
    return local_mean + lee_gain * (intensity - local_mean)


def band_sibling(holding, which_half, bit_index):
    half_rows = holding.shape[0] // 2
    own_rows = lax.dynamic_slice_in_dim(holding, which_half * half_rows, half_rows, 0)
    outgoing = lax.dynamic_slice_in_dim(holding, (1 - which_half) * half_rows, half_rows, 0)
    other_rows = swapped(outgoing, "band", bit_index)
    return (own_rows, other_rows)


def pair_level(
    holding,
    beam_block,
    which_half,
    tree_level,
    sibling_fn,
    bit_index,
    offsets,
    fraction,
    tilt_angle,
):
    own_rows, other_rows = sibling_fn(holding, which_half, bit_index)
    first_child = jnp.where(which_half == 0, own_rows, other_rows)
    second_child = jnp.where(which_half == 0, other_rows, own_rows)
    beam_block = 2 * beam_block + which_half
    parent = merge_pair(
        first_child[None],
        second_child[None],
        tree_level,
        beam_block * holding.shape[0],
        offsets,
        fraction,
        tilt_angle,
    )
    return (parent[0], beam_block)


def body(raw_echoes, pulse_order, matched, offsets, fraction, tilt_angle):
    pulse_rows = pulse_order.reshape(-1)
    pulse_count = pulse_rows.shape[0]
    freq_local = raw_echoes.shape[2]
    freq_start = lax.axis_index("band") * freq_local
    dft_table = range_table(
        lax.dynamic_slice_in_dim(matched, freq_start, freq_local, 1), freq_start, R
    )
    local_rows = raw_echoes.reshape(raw_echoes.shape[0], 2 * freq_local)
    own_profiles = sent_and_summed(
        jnp.dot(local_rows, dft_table, preferred_element_type=jnp.float32), "band", 0
    )
    profiles = own_profiles[pulse_rows].reshape(pulse_count, 2, R)
    images = profiles.reshape(pulse_count, 1, 2, R)
    local_levels = pulse_count.bit_length() - 1
    for tree_level in range(local_levels):
        images = merge_pair(
            images[0::2], images[1::2], tree_level, 0, offsets, fraction, tilt_angle
        )
    holding = images[0]
    tree_level = local_levels
    band_bits = lax.axis_size("band").bit_length() - 1
    aperture_bits = lax.axis_size("aperture").bit_length() - 1
    beam_block = jnp.int32(0)
    band_position = lax.axis_index("band")
    for bit_index in range(band_bits):
        which_half = band_position // 2**bit_index % 2
        holding, beam_block = pair_level(
            holding,
            beam_block,
            which_half,
            tree_level,
            band_sibling,
            bit_index,
            offsets,
            fraction,
            tilt_angle,
        )
        tree_level += 1
    aperture_position = lax.axis_index("aperture")
    aperture_count = lax.axis_size("aperture")
    each_rows = pulse_count // aperture_count
    reversal = []
    for member in range(aperture_count):
        flipped = 0
        for bit_index in range(aperture_bits):
            flipped = flipped + (member >> bit_index & 1) * 2 ** (aperture_bits - 1 - bit_index)
        reversal.append(flipped)
    reversal = np.array(reversal, dtype=np.int32)
    grouped = holding.reshape(aperture_count, each_rows, 2, R)[reversal]
    images = lax.all_to_all(grouped, "aperture", split_axis=0, concat_axis=0, tiled=True)
    reversed_position = jnp.int32(0)
    for bit_index in range(aperture_bits):
        reversed_position = reversed_position + aperture_position // 2**bit_index % 2 * 2 ** (
            aperture_bits - 1 - bit_index
        )
    final_block = beam_block * aperture_count + reversed_position
    for step_index in range(aperture_bits):
        beam_start = final_block * each_rows * 2 ** (step_index + 1)
        images = merge_pair(
            images[0::2], images[1::2], tree_level, beam_start, offsets, fraction, tilt_angle
        )
        tree_level += 1
    holding = images[0]
    intensity = holding[:, 0] ** 2 + holding[:, 1] ** 2
    return speckle(intensity[None])[0]


def solution(mesh):
    in_specs = (P("aperture", None, "band"), P("aperture", "band", None), P(), P(), P(), P())
    out_specs = P(("band", "aperture"), None)
    return jax.shard_map(body, mesh=mesh, in_specs=in_specs, out_specs=out_specs, check_vma=False)
```

profile of v0, /device:TPU:1, one launch (start us, length us, event | category | flops | bytes accessed | tf_op | source)
XLA Modules:
  0.0 257.7 jit_solution(12719882363145706004)
XLA Ops:
  0.0 1.1 copy.280
  3.0 1.0 copy.145
  4.0 10.2 %all-to-all-start = ((f32[16,32,256]{2,1,0:T(8,128)}), f32[16,32,256]{2,1,0:T(8,128)S(1)}, u32[]{:S(2)}, u32[]{:S(2)}) async-start(f32[16,32,256]{2,1,0:T(8,128)} %bitcast.3), calls=%async_computation | async-start | bytes 1048576 | tf_op jit(solution)/shard_map/all_to_all | solution.py:30
  95.2 1.0 fusion.465
  99.5 0.9 fusion.463
  100.7 1.0 fusion.529
  101.7 1.0 fusion.525
  102.7 0.9 fusion.527
  106.8 0.9 fusion.521
  109.9 0.9 convolution_bitcast_fusion.28
  110.8 0.9 convolution_bitcast_fusion.26
  112.1 2.2 collective-permute-start
  122.8 1.0 convolution_bitcast_fusion.23
  126.8 3.4 %collective-permute-start.1 = (f32[16,2,128]{2,0,1:T(8,128)S(1)}, f32[16,2,128]{2,0,1:T(8,128)S(1)}, u32[]{:S(2)}, u32[]{:S(2)}) collective-permute-start(f32[16,2,128]{2,0,1:T(8,128)S(1)} %constant_dynamic-slice_fusion.5), channel_id=1, source_target_pairs={{0,64},{32,96},{64,0},{96,32},{128,192},{160,224},{192,128},{224,1... | collective-permute-start | bytes 49160 | tf_op jit(solution)/shard_map/ppermute | solution.py:20
  138.1 1.0 convolution_bitcast_fusion.19
  139.1 0.9 convolution_bitcast_fusion.17
  140.0 1.0 convolution_bitcast_fusion.20
  142.2 4.2 %collective-permute-start.2 = (f32[16,2,128]{2,0,1:T(8,128)S(1)}, f32[16,2,128]{2,0,1:T(8,128)S(1)}, u32[]{:S(2)}, u32[]{:S(2)}) collective-permute-start(f32[16,2,128]{2,0,1:T(8,128)S(1)} %constant_dynamic-slice_fusion.3), channel_id=1, source_target_pairs={{0,128},{32,160},{64,192},{96,224},{128,0},{160,32},{192,64},{224,... | collective-permute-start | bytes 49160 | tf_op jit(solution)/shard_map/ppermute | solution.py:20
  154.2 0.9 convolution_bitcast_fusion.15
  158.1 4.4 %collective-permute-start.3 = (f32[16,2,128]{2,0,1:T(8,128)S(1)}, f32[16,2,128]{2,0,1:T(8,128)S(1)}, u32[]{:S(2)}, u32[]{:S(2)}) collective-permute-start(f32[16,2,128]{2,0,1:T(8,128)S(1)} %constant_dynamic-slice_fusion.1), channel_id=1, source_target_pairs={{0,256},{32,288},{64,320},{96,352},{128,384},{160,416},{192,448},{... | collective-permute-start | bytes 49160 | tf_op jit(solution)/shard_map/ppermute | solution.py:20
  211.4 1.0 convolution_bitcast_fusion.9
  214.5 1.2 gather_fusion.1
  215.7 11.2 %all-to-all-start.1 = ((f32[32,1,2,128]{3,2,1,0:T(2,128)}), f32[32,1,2,128]{3,2,1,0:T(2,128)S(1)}, u32[]{:S(2)}, u32[]{:S(2)}) async-start(f32[32,1,2,128]{3,2,1,0:T(2,128)} %bitcast.289), calls=%async_computation.1 | async-start | bytes 65536 | tf_op jit(solution)/shard_map/all_to_all | solution.py:209
  227.6 8.1 %all-to-all-done.1 = f32[32,1,2,128]{3,2,1,0:T(2,128)S(1)} async-done(((f32[32,1,2,128]{3,2,1,0:T(2,128)}), f32[32,1,2,128]{3,2,1,0:T(2,128)S(1)}, u32[]{:S(2)}, u32[]{:S(2)}) %all-to-all-start.1) | async-done | bytes 32800 | tf_op jit(solution)/shard_map/all_to_all | solution.py:209
  237.8 0.9 convolution_bitcast_fusion.5
  242.6 0.9 fusion.489
  244.3 0.9 fusion.483
  245.3 1.0 fusion.485
  247.2 0.9 fusion.481
  248.6 1.0 fusion.475
  253.5 0.9 convolution_bitcast_fusion.1
  254.4 1.0 convolution_bitcast_fusion.4
  (273 shorter events, 78.6 us)
Async XLA Ops:
  4.0 86.7 %all-to-all-start = ((f32[16,32,256]{2,1,0:T(8,128)}), f32[16,32,256]{2,1,0:T(8,128)S(1)}, u32[]{:S(2)}, u32[]{:S(2)}) async-start(f32[16,32,256]{2,1,0:T(8,128)} %bitcast.3), calls=%async_computation | async-start | bytes 1048576 | tf_op jit(solution)/shard_map/all_to_all | solution.py:30
  14.2 0.7 copy-start
  17.3 0.7 copy-start.2
  73.1 0.8 copy-start.4
  86.2 0.7 copy-start.3
  86.9 0.7 copy-start.1
  112.1 10.7 %collective-permute-start = (f32[16,2,128]{2,0,1:T(8,128)S(1)}, f32[16,2,128]{2,0,1:T(8,128)S(1)}, u32[]{:S(2)}, u32[]{:S(2)}) collective-permute-start(f32[16,2,128]{2,0,1:T(8,128)S(1)} %constant_dynamic-slice_fusion.7), channel_id=1, source_target_pairs={{0,32},{32,0},{64,96},{96,64},{128,160},{160,128},{192,224},{224,1... | collective-permute-start | bytes 49160 | tf_op jit(solution)/shard_map/ppermute | solution.py:20
  126.8 11.3 %collective-permute-start.1 = (f32[16,2,128]{2,0,1:T(8,128)S(1)}, f32[16,2,128]{2,0,1:T(8,128)S(1)}, u32[]{:S(2)}, u32[]{:S(2)}) collective-permute-start(f32[16,2,128]{2,0,1:T(8,128)S(1)} %constant_dynamic-slice_fusion.5), channel_id=1, source_target_pairs={{0,64},{32,96},{64,0},{96,32},{128,192},{160,224},{192,128},{224,1... | collective-permute-start | bytes 49160 | tf_op jit(solution)/shard_map/ppermute | solution.py:20
  142.2 11.9 %collective-permute-start.2 = (f32[16,2,128]{2,0,1:T(8,128)S(1)}, f32[16,2,128]{2,0,1:T(8,128)S(1)}, u32[]{:S(2)}, u32[]{:S(2)}) collective-permute-start(f32[16,2,128]{2,0,1:T(8,128)S(1)} %constant_dynamic-slice_fusion.3), channel_id=1, source_target_pairs={{0,128},{32,160},{64,192},{96,224},{128,0},{160,32},{192,64},{224,... | collective-permute-start | bytes 49160 | tf_op jit(solution)/shard_map/ppermute | solution.py:20
  158.1 52.4 %collective-permute-start.3 = (f32[16,2,128]{2,0,1:T(8,128)S(1)}, f32[16,2,128]{2,0,1:T(8,128)S(1)}, u32[]{:S(2)}, u32[]{:S(2)}) collective-permute-start(f32[16,2,128]{2,0,1:T(8,128)S(1)} %constant_dynamic-slice_fusion.1), channel_id=1, source_target_pairs={{0,256},{32,288},{64,320},{96,352},{128,384},{160,416},{192,448},{... | collective-permute-start | bytes 49160 | tf_op jit(solution)/shard_map/ppermute | solution.py:20
  215.7 20.0 %all-to-all-start.1 = ((f32[32,1,2,128]{3,2,1,0:T(2,128)}), f32[32,1,2,128]{3,2,1,0:T(2,128)S(1)}, u32[]{:S(2)}, u32[]{:S(2)}) async-start(f32[32,1,2,128]{3,2,1,0:T(2,128)} %bitcast.289), calls=%async_computation.1 | async-start | bytes 65536 | tf_op jit(solution)/shard_map/all_to_all | solution.py:209
where the time goes:
time: 261 us; the launch traced here: 258 us
  between operations  111 us (43%)
  matrix products  50.5 us (19%)
  other arithmetic  37.8 us (14%)
  starting transfers between devices  35.5 us (14%)
  local copies, waits for them, and re-layouts  14.2 us (5%)
  waiting for transfers between devices  8.12 us (3%)
    dot_general x56, matrix products, merge_pair(): shifted = jnp.einsum('nrckw,wo->nrcko', stacked, kernel, precision=HIGHEST)  50.2 us
    sin x48, other arithmetic, merge_pair(): sine_part = jnp.sin(phase_angle)[None, :, None]  31.9 us
    ppermute x4, starting transfers between devices, swapped(): return lax.ppermute(value, axis, pairs)  14.1 us
    all_to_all x1, starting transfers between devices, body(): lax.all_to_all(grouped, 'aperture', split_axis=0, concat_axis=0, tiled=True)  11.2 us
    all_to_all x1, starting transfers between devices, sent_and_summed(): pieces = lax.all_to_all(split_up(x, dim, peers), axis, 0, 0, tiled=True)  10.2 us
    all_to_all x1, waiting for transfers between devices, body(): lax.all_to_all(grouped, 'aperture', split_axis=0, concat_axis=0, tiled=True)  8.11 us
  transfers between devices with their start and end apart: 6, of which 1 were waited for; matrix products, arithmetic and copies ran while one was open for 15% of the time, Pallas kernels for 0%

commit v1 on v0

v1 whole, which is shorter than its diff:
```python
import functools
import math

import jax
import jax.numpy as jnp
from jax import lax
from jax.experimental import pallas as pl
from jax.experimental.pallas import tpu as pltpu
from jax.sharding import PartitionSpec as P

LEVELS = 14
F32 = jnp.float32
BF16 = jnp.bfloat16
MESH = pl.DeviceIdType.MESH


def bit_reversed(value, bits):
    return sum(((value >> t) & 1) << (bits - 1 - t) for t in range(bits))


def sin_cos(angle):
    turns = jnp.floor(angle * (2.0 / math.pi) + 0.5)
    rest = (angle - turns * 1.5707964) - turns * (-4.371139e-08)
    sq = rest * rest
    sine = rest + rest * sq * (
        -1.0 / 6 + sq * (1.0 / 120 + sq * (-1.0 / 5040 + sq * (1.0 / 362880)))
    )
    cosine = 1.0 + sq * (-0.5 + sq * (1.0 / 24 + sq * (-1.0 / 720 + sq * (1.0 / 40320))))
    size = jnp.abs(turns)
    odd = size == 1.0
    flip = jnp.where(size == 2.0, -1.0, 1.0)
    return (
        jnp.where(odd, turns * cosine, flip * sine),
        jnp.where(odd, -turns * sine, flip * cosine),
    )


def iota(shape, dim):
    return lax.broadcasted_iota(jnp.int32, shape, dim)


def bf16_pair(value):
    high = value.astype(BF16)
    low = (value - high.astype(F32)).astype(BF16)
    return high, low


def kernel(
    x_hbm, order_ref, matched_ref, offs_ref, frac_ref, tilt_ref, out_ref,
    xv, table, prods, own, other, from_core, partial, blocks,
    taps, phases, held, beams_out, beams_in, rows_out, rows_in, padded,
    x_sem, core_send, core_recv, blk_send, blk_recv, beam_send, beam_recv, row_send, row_recv,
):
    band = lax.axis_index("band")
    aperture = lax.axis_index("aperture")
    parity_word = band | (aperture << 4)
    child_word = parity_word << 5

    loads = []
    for pos in range(16):
        rel = 2 * pos + 1 if pos < 8 else 2 * (pos - 8)
        load = pltpu.make_async_copy(x_hbm.at[band ^ rel], xv.at[pos], x_sem.at[pos])
        load.start()
        loads.append(load)

    barrier = pltpu.get_barrier_semaphore()
    for rel in range(1, 16):
        pl.semaphore_signal(barrier, 1, device_id={"band": band ^ rel}, device_id_type=MESH)
    for rel in range(1, 32):
        pl.semaphore_signal(barrier, 1, device_id={"aperture": aperture ^ rel}, device_id_type=MESH)

    bins = iota((128, 128), 0).astype(F32)
    for half in range(2):
        start = pl.multiple_of(band * 256 + 128 * half, 128)
        freq = (start + iota((128, 128), 1)).astype(F32)
        turns = freq * bins
        turns = turns - 4096.0 * jnp.floor(turns * (1.0 / 4096) + 0.5)
        sine, cosine = sin_cos(turns * (2.0 * math.pi / 4096))
        spec_re = matched_ref[0:1, pl.ds(start, 128)]
        spec_im = matched_ref[1:2, pl.ds(start, 128)]
        real = (spec_re * cosine - spec_im * sine) * (1.0 / 64)
        imag = (spec_re * sine + spec_im * cosine) * (1.0 / 64)
        table[2 * half, 0:128] = real.astype(BF16)
        table[2 * half, 128:256] = imag.astype(BF16)
        table[2 * half + 1, 0:128] = (-imag).astype(BF16)
        table[2 * half + 1, 128:256] = real.astype(BF16)

    for chunk in range(4):
        for pos in range(4 * chunk, 4 * chunk + 4):
            loads[pos].wait()
        echoes = xv[4 * chunk : 4 * chunk + 4].reshape(512, 128)
        for kind in range(4):
            prod = lax.dot_general(
                echoes, table[kind], (((1,), (1,)), ((), ())), preferred_element_type=F32
            )
            prods[kind, 0] = prod[:, 0:128]
            prods[kind, 1] = prod[:, 128:256]
        target = other if chunk < 2 else own
        base = 4 * (chunk % 2)
        for part in range(2):
            total = prods[0, part, pl.ds(0, 128, stride=4), :]
            for kind in range(1, 4):
                total = total + prods[kind, part, pl.ds(kind, 128, stride=4), :]
            target[base : base + 4, :, 128 * part : 128 * part + 128] = total.reshape(4, 32, 128)

    pl.semaphore_wait(barrier, 46)

    order_far = (4, 3, 5, 2, 6, 7, 1, 0)
    core_copies = {}
    for j in order_far:
        copy = pltpu.make_async_remote_copy(
            src_ref=other.at[j], dst_ref=from_core.at[j],
            send_sem=core_send.at[j], recv_sem=core_recv.at[j],
            device_id={"band": band ^ 1}, device_id_type=MESH,
        )
        copy.start()
        core_copies[j] = copy
    blk_copies = []
    for j in order_far:
        core_copies[j].wait_recv()
        summed = (own[j] + from_core[j]).astype(BF16)
        if j == 0:
            blocks[0] = summed
            continue
        partial[j] = summed
        copy = pltpu.make_async_remote_copy(
            src_ref=partial.at[j], dst_ref=blocks.at[j],
            send_sem=blk_send.at[j], recv_sem=blk_recv.at[j],
            device_id={"band": band ^ (2 * j)}, device_id_type=MESH,
        )
        copy.start()
        blk_copies.append(copy)

    lane = iota((8, 128), 1)
    signed_lane = jnp.where(lane < 64, lane, lane - 128)
    lane8 = lane
    row8 = iota((8, 128), 0)

    @pl.loop(0, LEVELS)
    def _(level):
        parity_flip = (parity_word >> level) & 1
        child_flip = (child_word >> level) & 1
        for child in range(2):
            for half in range(2):
                offset = offs_ref[child ^ child_flip, half ^ parity_flip, 0, level]
                shift = frac_ref[child ^ child_flip, half ^ parity_flip, level]
                whole = 8 - offset - signed_lane
                dist = whole.astype(F32) - shift
                fracs = jnp.full((8, 128), math.pi, F32) * shift
                sq = fracs * fracs
                sine = fracs * (1.0 + sq * (-1.0 / 6 + sq * (1.0 / 120 + sq * (-1.0 / 5040 + sq * (1.0 / 362880 - sq * (1.0 / 39916800))))))
                sine = jnp.where((whole & 1) == 0, -sine, sine)
                zero = dist == 0.0
                sinc = jnp.where(zero, 1.0, sine / jnp.where(zero, 1.0, dist * math.pi))
                scaled = dist * (1.0 / 2.5)
                weight = sinc * jnp.exp(-(scaled * scaled)) * math.sqrt(0.5)
                weight = jnp.where(jnp.abs(dist) <= 4.0, weight, 0.0)
                strips = []
                for strip in range(16):
                    turned = pltpu.roll(weight, 8 * strip, 1, stride=1, stride_axis=0)
                    source = row8 + 8 * strip
                    window = source + 8 - offset
                    keep = (jnp.abs(lane8 - source) < 64) & (window >= 0) & (window < 128)
                    strips.append(jnp.where(keep, turned, 0.0))
                matrix = jnp.concatenate(strips, axis=0)
                high, low = bf16_pair(matrix)
                taps[level, child, 0:128, 128 * half : 128 * half + 128] = high
                taps[level, child, 128:256, 128 * half : 128 * half + 128] = low

    index = iota((32, 128), 0)
    row = index & 15
    half_bit = index >> 4
    for level in range(LEVELS):
        beam = half_bit ^ ((parity_word >> level) & 1)
        for t in range(level):
            if level <= 4 or (level <= 8 and t >= 4):
                bit = ((row >> (4 - level + t)) & 1) ^ ((parity_word >> t) & 1)
            elif t >= 9:
                bit = (row >> (level - 1 - t)) & 1
            else:
                bit = (parity_word >> t) & 1
            beam = beam + (bit << (level - t))
        position = 2.0 * (beam.astype(F32) + 0.5) / 2.0 ** (level + 1) - 1.0
        for child in range(2):
            angle = tilt_ref[child ^ ((child_word >> level) & 1), level] * position
            sine, cosine = sin_cos(angle)
            phases[level, child, 0] = cosine
            phases[level, child, 1] = sine

    padded[...] = jnp.zeros_like(padded)

    place = iota((32, 32), 0)
    pulse = ((place & 15) << 1) | (place >> 4)
    order = jnp.broadcast_to(order_ref[0:1, :].astype(F32), (32, 32))
    column = jnp.sum(jnp.where(iota((32, 32), 1) == pulse, order, 0.0), axis=1, keepdims=True)
    chosen = (iota((32, 256), 1) & 31).astype(F32)
    picker = jnp.where(chosen == column, 1.0, 0.0).astype(BF16)

    def merged(level, children):
        turned = []
        for child in range(2):
            high, low = bf16_pair(children[child])
            left = jnp.concatenate(
                [jnp.concatenate([high, high], axis=1), jnp.concatenate([low, low], axis=1)], axis=0
            )
            both = jnp.dot(left, taps[level, child], preferred_element_type=F32)
            shifted = both[0:32] + both[32:64]
            parts = []
            for half in range(2):
                real = shifted[0:16, 128 * half : 128 * half + 128]
                imag = shifted[16:32, 128 * half : 128 * half + 128]
                cosine = phases[level, child, 0, 16 * half : 16 * half + 16]
                sine = phases[level, child, 1, 16 * half : 16 * half + 16]
                parts.append((real * cosine - imag * sine, real * sine + imag * cosine))
            turned.append(parts)
        return [
            tuple(turned[0][half][part] + turned[1][half][part] for part in range(2))
            for half in range(2)
        ]

    def kept(parents):
        for half in range(2):
            for part in range(2):
                held[part, 16 * half : 16 * half + 16] = parents[half][part]
        return [
            jnp.concatenate([held[part, pl.ds(child, 16, stride=2), :] for part in range(2)], axis=0)
            for child in range(2)
        ]

    for copy in blk_copies:
        copy.wait_recv()
    profiles = jnp.dot(picker, blocks[...].reshape(256, 256), preferred_element_type=F32)
    children = [
        jnp.concatenate(
            [profiles[16 * c : 16 * c + 16, 0:128], profiles[16 * c : 16 * c + 16, 128:256]], axis=0
        )
        for c in range(2)
    ]
    for level in range(4):
        children = kept(merged(level, children))
    parents = merged(4, children)

    flat_out = beams_out.reshape(64, 128)
    flat_in = beams_in.reshape(64, 128)
    for half in range(2):
        for part in range(2):
            flat_out[pl.ds(2 * half + part, 16, stride=4), :] = parents[half][part]
            flat_in[2 * half + part : 2 * half + part + 1, :] = parents[half][part][0:1]
    beam_copies = []
    for rel in (8, 9, 6, 7, 10, 11, 4, 5, 12, 13, 14, 15, 2, 3, 1):
        copy = pltpu.make_async_remote_copy(
            src_ref=beams_out.at[rel], dst_ref=beams_in.at[rel],
            send_sem=beam_send.at[rel], recv_sem=beam_recv.at[rel],
            device_id={"band": band ^ rel}, device_id_type=MESH,
        )
        copy.start()
        beam_copies.append(copy)
    for copy in beam_copies:
        copy.wait_recv()
    children = [
        jnp.concatenate(
            [
                flat_in[pl.ds(4 * child + 2 * half + part, 8, stride=8), :]
                for part in range(2)
                for half in range(2)
            ],
            axis=0,
        )
        for child in range(2)
    ]
    for level in range(5, 8):
        children = kept(merged(level, children))
    parents = merged(8, children)

    flat_out = rows_out.reshape(64, 128)
    flat_in = rows_in.reshape(64, 128)
    for half in range(2):
        for part in range(2):
            flat_out[pl.ds(32 * half + part, 16, stride=2), :] = parents[half][part]
    for part in range(2):
        flat_in[part : part + 1, :] = parents[0][part][0:1]
    row_copies = []
    for rel in sorted(range(1, 32), key=lambda r: -min(r & 7, 8 - (r & 7)) - min(r >> 3, 4 - (r >> 3))):
        copy = pltpu.make_async_remote_copy(
            src_ref=rows_out.at[rel], dst_ref=rows_in.at[bit_reversed(rel, 5)],
            send_sem=row_send.at[rel], recv_sem=row_recv.at[rel],
            device_id={"aperture": aperture ^ rel}, device_id_type=MESH,
        )
        copy.start()
        row_copies.append(copy)
    for copy in row_copies:
        copy.wait_recv()
    children = [
        jnp.concatenate(
            [flat_in[pl.ds(32 * child + part, 16, stride=2), :] for part in range(2)], axis=0
        )
        for child in range(2)
    ]
    for level in range(9, 13):
        parents = merged(level, children)
        for half in range(2):
            for part in range(2):
                held[part, pl.ds(half, 16, stride=2), :] = parents[half][part]
        children = [
            jnp.concatenate([held[part, 16 * child : 16 * child + 16] for part in range(2)], axis=0)
            for child in range(2)
        ]
    parents = merged(13, children)
    for half in range(2):
        padded[pl.ds(8 + half, 16, stride=2), :] = parents[half][0] ** 2 + parents[half][1] ** 2

    middle = padded[8:40]
    sums = padded[6:38]
    squares = sums * sums
    for shift in range(1, 5):
        value = padded[6 + shift : 38 + shift]
        sums = sums + value
        squares = squares + value * value
    lanes = iota((32, 128), 1)

    def across(value):
        total = value
        for shift in (1, 2):
            total = total + jnp.where(lanes >= shift, pltpu.roll(value, shift, 1), 0.0)
            total = total + jnp.where(lanes < 128 - shift, pltpu.roll(value, 128 - shift, 1), 0.0)
        return total

    count_rows = jnp.minimum(index + 2, 31) - jnp.maximum(index - 2, 0) + 1
    count_lanes = jnp.minimum(lanes + 2, 127) - jnp.maximum(lanes - 2, 0) + 1
    count = (count_rows * count_lanes).astype(F32)
    mean = across(sums) / count
    square = across(squares) / count
    gain = (square - mean * mean) / (square - 0.75 * mean * mean + 0.001)
    out_ref[...] = mean + gain * (middle - mean)

    for copy in list(core_copies.values()) + blk_copies + beam_copies + row_copies:
        copy.wait_send()


def body(raw_echoes, pulse_order, matched, offsets, fraction, tilt_angle):
    echoes = raw_echoes.reshape(512, 2, 2, 128).transpose(0, 2, 1, 3).reshape(16, 128, 128)
    dma = pltpu.SemaphoreType.DMA
    vmem = pl.BlockSpec(memory_space=pltpu.VMEM)
    smem = pl.BlockSpec(memory_space=pltpu.SMEM)
    return pl.pallas_call(
        kernel,
        out_shape=jax.ShapeDtypeStruct((32, 128), F32),
        in_specs=[pl.BlockSpec(memory_space=pl.ANY), vmem, vmem, smem, smem, smem],
        out_specs=vmem,
        scratch_shapes=[
            pltpu.VMEM((16, 128, 128), BF16),
            pltpu.VMEM((4, 256, 128), BF16),
            pltpu.VMEM((4, 2, 512, 128), F32),
            pltpu.VMEM((8, 32, 256), F32),
            pltpu.VMEM((8, 32, 256), F32),
            pltpu.VMEM((8, 32, 256), F32),
            pltpu.VMEM((8, 32, 256), BF16),
            pltpu.VMEM((8, 32, 256), BF16),
            pltpu.VMEM((LEVELS, 2, 256, 256), BF16),
            pltpu.VMEM((LEVELS, 2, 2, 32, 128), F32),
            pltpu.VMEM((2, 32, 128), F32),
            pltpu.VMEM((16, 4, 128), F32),
            pltpu.VMEM((16, 4, 128), F32),
            pltpu.VMEM((32, 2, 128), F32),
            pltpu.VMEM((32, 2, 128), F32),
            pltpu.VMEM((48, 128), F32),
            dma((16,)), dma((8,)), dma((8,)), dma((8,)), dma((8,)),
            dma((16,)), dma((16,)), dma((32,)), dma((32,)),
        ],
        compiler_params=pltpu.CompilerParams(collective_id=0, has_side_effects=True),
    )(
        echoes,
        pulse_order.reshape(1, 32),
        matched,
        offsets.transpose(1, 2, 3, 0),
        fraction.transpose(1, 2, 0),
        tilt_angle.transpose(1, 0),
    )


def solution(mesh):
    in_specs = (P("aperture", None, "band"), P("aperture", "band", None), P(), P(), P(), P())
    out_specs = P(("band", "aperture"), None)
    return jax.shard_map(body, mesh=mesh, in_specs=in_specs, out_specs=out_specs, check_vma=False)
```

time: 261 us -> 38.7 us (0.15); the launches traced: 258 us -> 38.4 us
  between operations: 111 us -> 0.01 us
  matrix products: 50.5 us -> 0 us
  other arithmetic: 37.8 us -> 0 us
  Pallas kernels: 0 us -> 37.1 us
  starting transfers between devices: 35.5 us -> 0 us
  local copies, waits for them, and re-layouts: 14.2 us -> 1.32 us
  waiting for transfers between devices: 8.12 us -> 0 us
    dot_general x57 -> x0, matrix products: 50.5 us -> none  [the longest x56 50.2 us: merge_pair(): shifted = jnp.einsum('nrckw,wo->nrcko', stacked, kernel, precision=HIGHEST)]
    pallas_call x0 -> x1, Pallas kernels: none -> 37.1 us  [body(): pl.pallas_call(kernel, out_shape=jax.ShapeDtypeStruct((32, 128), F32), in...]
    sin x48 -> x0, other arithmetic: 31.9 us -> none  [merge_pair(): sine_part = jnp.sin(phase_angle)[None, :, None]]
    all_to_all x2 -> x0, starting transfers between devices: 21.4 us -> none  [the longest x1 11.2 us: body(): lax.all_to_all(grouped, 'aperture', split_axis=0, concat_axis=0, tiled=True)]
    ppermute x4 -> x0, starting transfers between devices: 14.1 us -> none  [swapped(): return lax.ppermute(value, axis, pairs)]
    all_to_all x2 -> x0, waiting for transfers between devices: 8.11 us -> none  [the longest x1 8.11 us: body(): lax.all_to_all(grouped, 'aperture', split_axis=0, concat_axis=0, tiled=True)]
    slice x25 -> x0, local copies, waits for them, and re-layouts: 7.41 us -> none  [the longest x3 2.18 us: merge_pair(): kernel = interp_kernel(fraction[tree_level, child_index, parity])]
    another operation x70 -> x0, other arithmetic: 4.61 us -> none  [the longest x57 3.89 us: merge_pair(): jnp.stack([real_part * cosine - imag_part * sine_part, real_part * sine_p...]
  transfers between devices with their start and end apart: 6 -> 0, of which waited for: 1 -> 0; matrix products, arithmetic and copies ran while one was open for 15% -> 0% of each run, Pallas kernels for 0% -> 0%
where the time goes in v1:
time: 38.7 us; the launch traced here: 38.4 us
  Pallas kernels  37.1 us (96%)
  local copies, waits for them, and re-layouts  1.32 us (3%)
    pallas_call x1, Pallas kernels, body(): pl.pallas_call(kernel, out_shape=jax.ShapeDtypeStruct((32, 128), F32), in...  37.1 us
    unnamed x1, local copies, waits for them, and re-layouts  1.32 us

profile of v1, /device:TPU:1, one launch (start us, length us, event | category | flops | bytes accessed | tf_op | source)
XLA Modules:
  0.0 38.4 jit_solution(16505506069058964452)
XLA Ops:
  0.0 37.1 %shard_map.64 = f32[32,128]{1,0:T(8,128)} custom-call(bf16[16,128,128]{2,1,0:T(8,128)(2,1)} %bitcast.9, s32[1,32]{1,0:T(1,128)} %bitcast.13, f32[2,4096]{1,0:T(2,128)} %matched_ref.1, s32[2,2,1,14]{3,2,1,0:T(1,128)} %bitcast.10, f32[2,2,14]{2,1,0:T(2,128)} %bitcast.11, f32[2,14]{1,0:T(2,128)} %bitcast.12), custom_call_target="tpu_custom_call" | custom-call | tf_op jit(solution)/shard_map/pallas_call | solution.py:345
  37.1 1.3 %copy.9 = f32[32,128]{1,0:T(8,128)} copy(f32[32,128]{1,0:T(8,128)} %shard_map.64) | data formatting | bytes 32768

commit v2 on v1

--- a/solution.py
+++ b/solution.py
@@ -46,15 +46,54 @@
 
 
 def kernel(
-    x_hbm, order_ref, matched_ref, offs_ref, frac_ref, tilt_ref, out_ref,
+    x_hbm, order_hbm, matched_hbm, offs_hbm, frac_hbm, tilt_hbm, out_ref,
+    order_ref, matched_ref, offs_ref, frac_ref, tilt_ref,
     xv, table, prods, own, other, from_core, partial, blocks,
     taps, phases, held, beams_out, beams_in, rows_out, rows_in, padded,
-    x_sem, core_send, core_recv, blk_send, blk_recv, beam_send, beam_recv, row_send, row_recv,
+    core_ready, band_ready, all_ready, arg_sem, x_sem, core_send, core_recv, blk_send, blk_recv, beam_send, beam_recv, row_send, row_recv,
 ):
     band = lax.axis_index("band")
     aperture = lax.axis_index("aperture")
     parity_word = band | (aperture << 4)
     child_word = parity_word << 5
+
+    on_first = (band & 1) == 0
+    on_second = (band & 1) == 1
+    speaker = band == 0
+    listener = on_first & (band > 0)
+    barrier = pltpu.get_barrier_semaphore()
+
+    def greet(peer):
+        pl.semaphore_signal(barrier, 1, device_id={"band": peer}, device_id_type=MESH)
+
+    def tell(semaphore, peer):
+        pl.semaphore_signal(semaphore, 1, device_id={"band": peer}, device_id_type=MESH)
+
+    @pl.when(on_first)
+    def _():
+        greet(band ^ 1)
+
+    for rel in range(2, 16, 2):
+        peer = (band & 14) ^ rel
+
+        @pl.when(peer > 0)
+        def _():
+            greet(peer)
+
+    start = pl.multiple_of(band * 256, 256)
+    args = [
+        pltpu.make_async_copy(source, target, arg_sem.at[i])
+        for i, (source, target) in enumerate(
+            (
+                (matched_hbm.at[:, pl.ds(start, 256)], matched_ref),
+                (order_hbm, order_ref),
+                (offs_hbm, offs_ref),
+                (frac_hbm, frac_ref),
+                (tilt_hbm, tilt_ref),
+            )
+        )
+    ]
+    args[0].start()
 
     loads = []
     for pos in range(16):
@@ -62,22 +101,18 @@
         load = pltpu.make_async_copy(x_hbm.at[band ^ rel], xv.at[pos], x_sem.at[pos])
         load.start()
         loads.append(load)
-
-    barrier = pltpu.get_barrier_semaphore()
-    for rel in range(1, 16):
-        pl.semaphore_signal(barrier, 1, device_id={"band": band ^ rel}, device_id_type=MESH)
-    for rel in range(1, 32):
-        pl.semaphore_signal(barrier, 1, device_id={"aperture": aperture ^ rel}, device_id_type=MESH)
+    for arg in args[1:]:
+        arg.start()
 
     bins = iota((128, 128), 0).astype(F32)
+    args[0].wait()
     for half in range(2):
-        start = pl.multiple_of(band * 256 + 128 * half, 128)
-        freq = (start + iota((128, 128), 1)).astype(F32)
+        freq = (start + 128 * half + iota((128, 128), 1)).astype(F32)
         turns = freq * bins
         turns = turns - 4096.0 * jnp.floor(turns * (1.0 / 4096) + 0.5)
         sine, cosine = sin_cos(turns * (2.0 * math.pi / 4096))
-        spec_re = matched_ref[0:1, pl.ds(start, 128)]
-        spec_im = matched_ref[1:2, pl.ds(start, 128)]
+        spec_re = matched_ref[0:1, 128 * half : 128 * half + 128]
+        spec_im = matched_ref[1:2, 128 * half : 128 * half + 128]
         real = (spec_re * cosine - spec_im * sine) * (1.0 / 64)
         imag = (spec_re * sine + spec_im * cosine) * (1.0 / 64)
         table[2 * half, 0:128] = real.astype(BF16)
@@ -85,7 +120,7 @@
         table[2 * half + 1, 0:128] = (-imag).astype(BF16)
         table[2 * half + 1, 128:256] = real.astype(BF16)
 
-    for chunk in range(4):
+    def compress(chunk, target):
         for pos in range(4 * chunk, 4 * chunk + 4):
             loads[pos].wait()
         echoes = xv[4 * chunk : 4 * chunk + 4].reshape(512, 128)
@@ -95,7 +130,6 @@
             )
             prods[kind, 0] = prod[:, 0:128]
             prods[kind, 1] = prod[:, 128:256]
-        target = other if chunk < 2 else own
         base = 4 * (chunk % 2)
         for part in range(2):
             total = prods[0, part, pl.ds(0, 128, stride=4), :]
@@ -103,18 +137,58 @@
                 total = total + prods[kind, part, pl.ds(kind, 128, stride=4), :]
             target[base : base + 4, :, 128 * part : 128 * part + 128] = total.reshape(4, 32, 128)
 
-    pl.semaphore_wait(barrier, 46)
-
     order_far = (4, 3, 5, 2, 6, 7, 1, 0)
     core_copies = {}
-    for j in order_far:
-        copy = pltpu.make_async_remote_copy(
-            src_ref=other.at[j], dst_ref=from_core.at[j],
-            send_sem=core_send.at[j], recv_sem=core_recv.at[j],
-            device_id={"band": band ^ 1}, device_id_type=MESH,
-        )
-        copy.start()
-        core_copies[j] = copy
+
+    def to_partner(slots):
+        for j in slots:
+            copy = pltpu.make_async_remote_copy(
+                src_ref=other.at[j], dst_ref=from_core.at[j],
+                send_sem=core_send.at[j], recv_sem=core_recv.at[j],
+                device_id={"band": band ^ 1}, device_id_type=MESH,
+            )
+            copy.start()
+            core_copies[j] = copy
+
+    compress(1, other)
+
+    @pl.when(on_second)
+    def _():
+        pl.semaphore_wait(barrier, 1)
+        tell(core_ready, band ^ 1)
+
+    @pl.when(on_first)
+    def _():
+        pl.semaphore_wait(core_ready, 1)
+
+    to_partner((4, 5, 6, 7))
+    compress(0, other)
+    to_partner((3, 2, 1, 0))
+    compress(3, own)
+    compress(2, own)
+
+    @pl.when(listener)
+    def _():
+        pl.semaphore_wait(barrier, 14)
+        tell(band_ready, band ^ 1)
+
+    @pl.when(band == 2)
+    def _():
+        tell(band_ready, 0)
+
+    @pl.when(speaker)
+    def _():
+        pl.semaphore_wait(band_ready, 1)
+        tell(band_ready, 1)
+        for rel in range(1, 32):
+            pl.semaphore_signal(
+                barrier, 1, device_id={"aperture": aperture ^ rel}, device_id_type=MESH
+            )
+
+    @pl.when(on_second)
+    def _():
+        pl.semaphore_wait(band_ready, 1)
+
     blk_copies = []
     for j in order_far:
         core_copies[j].wait_recv()
@@ -131,6 +205,8 @@
         copy.start()
         blk_copies.append(copy)
 
+    for arg in args[1:]:
+        arg.wait()
     lane = iota((8, 128), 1)
     signed_lane = jnp.where(lane < 64, lane, lane - 128)
     lane8 = lane
@@ -257,6 +333,13 @@
         beam_copies.append(copy)
     for copy in beam_copies:
         copy.wait_recv()
+
+    @pl.when(speaker)
+    def _():
+        pl.semaphore_wait(barrier, 31)
+        for rel in range(1, 16):
+            tell(all_ready, rel)
+
     children = [
         jnp.concatenate(
             [
@@ -271,6 +354,10 @@
     for level in range(5, 8):
         children = kept(merged(level, children))
     parents = merged(8, children)
+
+    @pl.when(band > 0)
+    def _():
+        pl.semaphore_wait(all_ready, 1)
 
     flat_out = rows_out.reshape(64, 128)
     flat_in = rows_in.reshape(64, 128)
@@ -340,14 +427,18 @@
 def body(raw_echoes, pulse_order, matched, offsets, fraction, tilt_angle):
     echoes = raw_echoes.reshape(512, 2, 2, 128).transpose(0, 2, 1, 3).reshape(16, 128, 128)
     dma = pltpu.SemaphoreType.DMA
-    vmem = pl.BlockSpec(memory_space=pltpu.VMEM)
-    smem = pl.BlockSpec(memory_space=pltpu.SMEM)
+    regular = pltpu.SemaphoreType.REGULAR
     return pl.pallas_call(
         kernel,
         out_shape=jax.ShapeDtypeStruct((32, 128), F32),
-        in_specs=[pl.BlockSpec(memory_space=pl.ANY), vmem, vmem, smem, smem, smem],
-        out_specs=vmem,
+        in_specs=[pl.BlockSpec(memory_space=pl.ANY)] * 6,
+        out_specs=pl.BlockSpec(memory_space=pltpu.VMEM),
         scratch_shapes=[
+            pltpu.VMEM((1, 32), jnp.int32),
+            pltpu.VMEM((2, 256), F32),
+            pltpu.SMEM((2, 2, 1, LEVELS), jnp.int32),
+            pltpu.SMEM((2, 2, LEVELS), F32),
+            pltpu.SMEM((2, LEVELS), F32),
             pltpu.VMEM((16, 128, 128), BF16),
             pltpu.VMEM((4, 256, 128), BF16),
             pltpu.VMEM((4, 2, 512, 128), F32),
@@ -364,7 +455,7 @@
             pltpu.VMEM((32, 2, 128), F32),
             pltpu.VMEM((32, 2, 128), F32),
             pltpu.VMEM((48, 128), F32),
-            dma((16,)), dma((8,)), dma((8,)), dma((8,)), dma((8,)),
+            regular, regular, regular, dma((5,)), dma((16,)), dma((8,)), dma((8,)), dma((8,)), dma((8,)),
             dma((16,)), dma((16,)), dma((32,)), dma((32,)),
         ],
         compiler_params=pltpu.CompilerParams(collective_id=0, has_side_effects=True),

time: 38.7 us -> 37.2 us (0.961)
  Pallas kernels: 37.1 us -> 35.6 us
    pallas_call x1, Pallas kernels: 37.1 us -> 35.6 us  [body(): pl.pallas_call(kernel, out_shape=jax.ShapeDtypeStruct((32, 128), F32), in...]
where the time goes in v2:
time: 37.2 us; the launch traced here: 36.9 us
  Pallas kernels  35.6 us (96%)
  local copies, waits for them, and re-layouts  1.32 us (4%)
    pallas_call x1, Pallas kernels, body(): pl.pallas_call(kernel, out_shape=jax.ShapeDtypeStruct((32, 128), F32), in...  35.6 us
    unnamed x1, local copies, waits for them, and re-layouts  1.32 us

profile of v2, /device:TPU:1, one launch (start us, length us, event | category | flops | bytes accessed | tf_op | source)
XLA Modules:
  0.0 36.9 jit_solution(7798506034129341196)
XLA Ops:
  0.0 35.6 %shard_map.64 = f32[32,128]{1,0:T(8,128)} custom-call(bf16[16,128,128]{2,1,0:T(8,128)(2,1)} %bitcast.9, s32[1,32]{1,0:T(1,128)} %bitcast.13, f32[2,4096]{1,0:T(2,128)} %matched_hbm.1, s32[2,2,1,14]{3,2,1,0:T(1,128)} %bitcast.10, f32[2,2,14]{2,1,0:T(2,128)} %bitcast.11, f32[2,14]{1,0:T(2,128)} %bitcast.12), custom_call_target="tpu_custom_call" | custom-call | tf_op jit(solution)/shard_map/pallas_call | solution.py:431
  35.6 1.3 %copy.9 = f32[32,128]{1,0:T(8,128)} copy(f32[32,128]{1,0:T(8,128)} %shard_map.64) | data formatting | bytes 32768

commit v3 on v2

--- a/solution.py
+++ b/solution.py
@@ -95,12 +95,12 @@
     ]
     args[0].start()
 
-    loads = []
-    for pos in range(16):
+    loads = {}
+    for pos in (4, 5, 6, 7, 0, 1, 2, 3, 12, 13, 14, 15, 8, 9, 10, 11):
         rel = 2 * pos + 1 if pos < 8 else 2 * (pos - 8)
         load = pltpu.make_async_copy(x_hbm.at[band ^ rel], xv.at[pos], x_sem.at[pos])
         load.start()
-        loads.append(load)
+        loads[pos] = load
     for arg in args[1:]:
         arg.start()
 
@@ -331,15 +331,14 @@
         )
         copy.start()
         beam_copies.append(copy)
-    for copy in beam_copies:
-        copy.wait_recv()
-
     @pl.when(speaker)
     def _():
         pl.semaphore_wait(barrier, 31)
         for rel in range(1, 16):
             tell(all_ready, rel)
 
+    for copy in beam_copies:
+        copy.wait_recv()
     children = [
         jnp.concatenate(
             [
@@ -430,7 +429,7 @@
     regular = pltpu.SemaphoreType.REGULAR
     return pl.pallas_call(
         kernel,
-        out_shape=jax.ShapeDtypeStruct((32, 128), F32),
+        out_shape=pltpu.VMEM((32, 128), F32),
         in_specs=[pl.BlockSpec(memory_space=pl.ANY)] * 6,
         out_specs=pl.BlockSpec(memory_space=pltpu.VMEM),
         scratch_shapes=[

time: 37.2 us -> 35.9 us (0.965)
  local copies, waits for them, and re-layouts: 1.32 us -> 0.61 us
  Pallas kernels: 35.6 us -> 35.1 us
    unnamed x1, local copies, waits for them, and re-layouts: 1.32 us -> 0.61 us
    pallas_call x1, Pallas kernels: 35.6 us -> 35.1 us  [body(): pl.pallas_call(kernel, out_shape=pltpu.VMEM((32, 128), F32), in_specs=[pl...]
where the time goes in v3:
time: 35.9 us; the launch traced here: 35.7 us
  Pallas kernels  35.1 us (98%)
  local copies, waits for them, and re-layouts  0.61 us (2%)
    pallas_call x1, Pallas kernels, body(): pl.pallas_call(kernel, out_shape=pltpu.VMEM((32, 128), F32), in_specs=[pl...  35.1 us

profile of v3, /device:TPU:1, one launch (start us, length us, event | category | flops | bytes accessed | tf_op | source)
XLA Modules:
  0.0 35.7 jit_solution(16790348673007298607)
XLA Ops:
  0.0 35.1 %shard_map.64 = f32[32,128]{1,0:T(8,128)S(1)} custom-call(bf16[16,128,128]{2,1,0:T(8,128)(2,1)} %bitcast.9, s32[1,32]{1,0:T(1,128)} %bitcast.13, f32[2,4096]{1,0:T(2,128)} %matched_hbm.1, s32[2,2,1,14]{3,2,1,0:T(1,128)} %bitcast.10, f32[2,2,14]{2,1,0:T(2,128)} %bitcast.11, f32[2,14]{1,0:T(2,128)} %bitcast.12), custom_call_target="tpu_custom_call" | custom-call | tf_op jit(solution)/shard_map/pallas_call | solution.py:430
  35.1 0.6 %copy.9 = f32[32,128]{1,0:T(8,128)} copy(f32[32,128]{1,0:T(8,128)S(1)} %shard_map.64) | data formatting | bytes 32768

commit v4 on v3

--- a/solution.py
+++ b/solution.py
@@ -98,11 +98,19 @@
     loads = {}
     for pos in (4, 5, 6, 7, 0, 1, 2, 3, 12, 13, 14, 15, 8, 9, 10, 11):
         rel = 2 * pos + 1 if pos < 8 else 2 * (pos - 8)
-        load = pltpu.make_async_copy(x_hbm.at[band ^ rel], xv.at[pos], x_sem.at[pos])
-        load.start()
-        loads[pos] = load
+        for half in range(2):
+            load = pltpu.make_async_copy(
+                x_hbm.at[band ^ rel, :, half], xv.at[half, pos], x_sem.at[half, pos]
+            )
+            load.start()
+            loads[half, pos] = load
     for arg in args[1:]:
         arg.start()
+
+    @pl.when(on_second)
+    def _():
+        pl.semaphore_wait(barrier, 1)
+        tell(core_ready, band ^ 1)
 
     bins = iota((128, 128), 0).astype(F32)
     args[0].wait()
@@ -115,27 +123,30 @@
         spec_im = matched_ref[1:2, 128 * half : 128 * half + 128]
         real = (spec_re * cosine - spec_im * sine) * (1.0 / 64)
         imag = (spec_re * sine + spec_im * cosine) * (1.0 / 64)
-        table[2 * half, 0:128] = real.astype(BF16)
-        table[2 * half, 128:256] = imag.astype(BF16)
-        table[2 * half + 1, 0:128] = (-imag).astype(BF16)
-        table[2 * half + 1, 128:256] = real.astype(BF16)
+        side = slice(128 * half, 128 * half + 128)
+        table[0, 0:128, side] = real.astype(BF16)
+        table[0, 128:256, side] = imag.astype(BF16)
+        table[1, 0:128, side] = (-imag).astype(BF16)
+        table[1, 128:256, side] = real.astype(BF16)
 
     def compress(chunk, target):
         for pos in range(4 * chunk, 4 * chunk + 4):
-            loads[pos].wait()
-        echoes = xv[4 * chunk : 4 * chunk + 4].reshape(512, 128)
-        for kind in range(4):
+            for half in range(2):
+                loads[half, pos].wait()
+        echoes = jnp.concatenate(
+            [xv.at[half].reshape(1024, 128)[256 * chunk : 256 * chunk + 256] for half in range(2)],
+            axis=1,
+        )
+        for part in range(2):
             prod = lax.dot_general(
-                echoes, table[kind], (((1,), (1,)), ((), ())), preferred_element_type=F32
-            )
-            prods[kind, 0] = prod[:, 0:128]
-            prods[kind, 1] = prod[:, 128:256]
+                echoes, table[part], (((1,), (1,)), ((), ())), preferred_element_type=F32
+            )
+            prods[part, 0] = prod[:, 0:128]
+            prods[part, 1] = prod[:, 128:256]
         base = 4 * (chunk % 2)
-        for part in range(2):
-            total = prods[0, part, pl.ds(0, 128, stride=4), :]
-            for kind in range(1, 4):
-                total = total + prods[kind, part, pl.ds(kind, 128, stride=4), :]
-            target[base : base + 4, :, 128 * part : 128 * part + 128] = total.reshape(4, 32, 128)
+        for out in range(2):
+            total = prods[0, out, pl.ds(0, 128, stride=2), :] + prods[1, out, pl.ds(1, 128, stride=2), :]
+            target[base : base + 4, :, 128 * out : 128 * out + 128] = total.reshape(4, 32, 128)
 
     order_far = (4, 3, 5, 2, 6, 7, 1, 0)
     core_copies = {}
@@ -152,11 +163,6 @@
 
     compress(1, other)
 
-    @pl.when(on_second)
-    def _():
-        pl.semaphore_wait(barrier, 1)
-        tell(core_ready, band ^ 1)
-
     @pl.when(on_first)
     def _():
         pl.semaphore_wait(core_ready, 1)
@@ -165,16 +171,20 @@
     compress(0, other)
     to_partner((3, 2, 1, 0))
     compress(3, own)
+
+    @pl.when(listener)
+    def _():
+        pl.semaphore_wait(barrier, 14)
+
+    @pl.when(band == 2)
+    def _():
+        tell(band_ready, 0)
+
+    @pl.when(listener)
+    def _():
+        tell(band_ready, band ^ 1)
+
     compress(2, own)
-
-    @pl.when(listener)
-    def _():
-        pl.semaphore_wait(barrier, 14)
-        tell(band_ready, band ^ 1)
-
-    @pl.when(band == 2)
-    def _():
-        tell(band_ready, 0)
 
     @pl.when(speaker)
     def _():
@@ -366,7 +376,7 @@
     for part in range(2):
         flat_in[part : part + 1, :] = parents[0][part][0:1]
     row_copies = []
-    for rel in sorted(range(1, 32), key=lambda r: -min(r & 7, 8 - (r & 7)) - min(r >> 3, 4 - (r >> 3))):
+    for rel in sorted(range(1, 32), key=lambda r: (-(r & 4), -min(r & 7, 8 - (r & 7)) - min(r >> 3, 4 - (r >> 3)))):
         copy = pltpu.make_async_remote_copy(
             src_ref=rows_out.at[rel], dst_ref=rows_in.at[bit_reversed(rel, 5)],
             send_sem=row_send.at[rel], recv_sem=row_recv.at[rel],
@@ -424,7 +434,7 @@
 
 
 def body(raw_echoes, pulse_order, matched, offsets, fraction, tilt_angle):
-    echoes = raw_echoes.reshape(512, 2, 2, 128).transpose(0, 2, 1, 3).reshape(16, 128, 128)
+    echoes = raw_echoes.reshape(512, 2, 2, 128).transpose(0, 2, 1, 3).reshape(16, 32, 2, 2, 128)
     dma = pltpu.SemaphoreType.DMA
     regular = pltpu.SemaphoreType.REGULAR
     return pl.pallas_call(
@@ -438,9 +448,9 @@
             pltpu.SMEM((2, 2, 1, LEVELS), jnp.int32),
             pltpu.SMEM((2, 2, LEVELS), F32),
             pltpu.SMEM((2, LEVELS), F32),
-            pltpu.VMEM((16, 128, 128), BF16),
-            pltpu.VMEM((4, 256, 128), BF16),
-            pltpu.VMEM((4, 2, 512, 128), F32),
+            pltpu.VMEM((2, 16, 32, 2, 128), BF16),
+            pltpu.VMEM((2, 256, 256), BF16),
+            pltpu.VMEM((2, 2, 256, 128), F32),
             pltpu.VMEM((8, 32, 256), F32),
             pltpu.VMEM((8, 32, 256), F32),
             pltpu.VMEM((8, 32, 256), F32),
@@ -454,7 +464,7 @@
             pltpu.VMEM((32, 2, 128), F32),
             pltpu.VMEM((32, 2, 128), F32),
             pltpu.VMEM((48, 128), F32),
-            regular, regular, regular, dma((5,)), dma((16,)), dma((8,)), dma((8,)), dma((8,)), dma((8,)),
+            regular, regular, regular, dma((5,)), dma((2, 16)), dma((8,)), dma((8,)), dma((8,)), dma((8,)),
             dma((16,)), dma((16,)), dma((32,)), dma((32,)),
         ],
         compiler_params=pltpu.CompilerParams(collective_id=0, has_side_effects=True),

time: 35.9 us -> 36 us (level)
  no operation moved by 1% of the time
where the time goes in v4:
time: 36 us; the launch traced here: 35.8 us
  Pallas kernels  35.2 us (98%)
  local copies, waits for them, and re-layouts  0.61 us (2%)
    pallas_call x1, Pallas kernels, body(): pl.pallas_call(kernel, out_shape=pltpu.VMEM((32, 128), F32), in_specs=[pl...  35.2 us

profile of v4, /device:TPU:1, one launch (start us, length us, event | category | flops | bytes accessed | tf_op | source)
XLA Modules:
  0.0 35.8 jit_solution(17026361294427425341)
XLA Ops:
  0.0 35.2 %shard_map.64 = f32[32,128]{1,0:T(8,128)S(1)} custom-call(bf16[16,32,2,2,128]{4,3,2,1,0:T(2,128)(2,1)} %bitcast.9, s32[1,32]{1,0:T(1,128)} %bitcast.13, f32[2,4096]{1,0:T(2,128)} %matched_hbm.1, s32[2,2,1,14]{3,2,1,0:T(1,128)} %bitcast.10, f32[2,2,14]{2,1,0:T(2,128)} %bitcast.11, f32[2,14]{1,0:T(2,128)} %bitcast.12), custom_call_target="tpu_custom_call" | custom-call | tf_op jit(solution)/shard_map/pallas_call | solution.py:440
  35.2 0.6 %copy.9 = f32[32,128]{1,0:T(8,128)} copy(f32[32,128]{1,0:T(8,128)S(1)} %shard_map.64) | data formatting | bytes 32768

commit v5 on v4

--- a/solution.py
+++ b/solution.py
@@ -106,11 +106,6 @@
             loads[half, pos] = load
     for arg in args[1:]:
         arg.start()
-
-    @pl.when(on_second)
-    def _():
-        pl.semaphore_wait(barrier, 1)
-        tell(core_ready, band ^ 1)
 
     bins = iota((128, 128), 0).astype(F32)
     args[0].wait()
@@ -163,6 +158,11 @@
 
     compress(1, other)
 
+    @pl.when(on_second)
+    def _():
+        pl.semaphore_wait(barrier, 1)
+        tell(core_ready, band ^ 1)
+
     @pl.when(on_first)
     def _():
         pl.semaphore_wait(core_ready, 1)
@@ -171,20 +171,16 @@
     compress(0, other)
     to_partner((3, 2, 1, 0))
     compress(3, own)
+    compress(2, own)
 
     @pl.when(listener)
     def _():
         pl.semaphore_wait(barrier, 14)
+        tell(band_ready, band ^ 1)
 
     @pl.when(band == 2)
     def _():
         tell(band_ready, 0)
-
-    @pl.when(listener)
-    def _():
-        tell(band_ready, band ^ 1)
-
-    compress(2, own)
 
     @pl.when(speaker)
     def _():
@@ -376,7 +372,7 @@
     for part in range(2):
         flat_in[part : part + 1, :] = parents[0][part][0:1]
     row_copies = []
-    for rel in sorted(range(1, 32), key=lambda r: (-(r & 4), -min(r & 7, 8 - (r & 7)) - min(r >> 3, 4 - (r >> 3)))):
+    for rel in sorted(range(1, 32), key=lambda r: -min(r & 7, 8 - (r & 7)) - min(r >> 3, 4 - (r >> 3))):
         copy = pltpu.make_async_remote_copy(
             src_ref=rows_out.at[rel], dst_ref=rows_in.at[bit_reversed(rel, 5)],
             send_sem=row_send.at[rel], recv_sem=row_recv.at[rel],

time: 36 us -> 35.9 us (level)
  no operation moved by 1% of the time
where the time goes in v5:
time: 35.9 us; the launch traced here: 35.7 us
  Pallas kernels  35.1 us (98%)
  local copies, waits for them, and re-layouts  0.61 us (2%)
    pallas_call x1, Pallas kernels, body(): pl.pallas_call(kernel, out_shape=pltpu.VMEM((32, 128), F32), in_specs=[pl...  35.1 us

profile of v5, /device:TPU:1, one launch (start us, length us, event | category | flops | bytes accessed | tf_op | source)
XLA Modules:
  0.0 35.7 jit_solution(5610943452325975407)
XLA Ops:
  0.0 35.1 %shard_map.64 = f32[32,128]{1,0:T(8,128)S(1)} custom-call(bf16[16,32,2,2,128]{4,3,2,1,0:T(2,128)(2,1)} %bitcast.9, s32[1,32]{1,0:T(1,128)} %bitcast.13, f32[2,4096]{1,0:T(2,128)} %matched_hbm.1, s32[2,2,1,14]{3,2,1,0:T(1,128)} %bitcast.10, f32[2,2,14]{2,1,0:T(2,128)} %bitcast.11, f32[2,14]{1,0:T(2,128)} %bitcast.12), custom_call_target="tpu_custom_call" | custom-call | tf_op jit(solution)/shard_map/pallas_call | solution.py:436
  35.1 0.6 %copy.9 = f32[32,128]{1,0:T(8,128)} copy(f32[32,128]{1,0:T(8,128)S(1)} %shard_map.64) | data formatting | bytes 32768

commit v6 on v3

--- a/solution.py
+++ b/solution.py
@@ -103,6 +103,11 @@
         loads[pos] = load
     for arg in args[1:]:
         arg.start()
+
+    @pl.when(on_second)
+    def _():
+        pl.semaphore_wait(barrier, 1)
+        tell(core_ready, band ^ 1)
 
     bins = iota((128, 128), 0).astype(F32)
     args[0].wait()
@@ -151,11 +156,6 @@
             core_copies[j] = copy
 
     compress(1, other)
-
-    @pl.when(on_second)
-    def _():
-        pl.semaphore_wait(barrier, 1)
-        tell(core_ready, band ^ 1)
 
     @pl.when(on_first)
     def _():

time: 35.9 us -> 35.9 us (level)
  no operation moved by 1% of the time
where the time goes in v6:
time: 35.9 us; the launch traced here: 35.7 us
  Pallas kernels  35.1 us (98%)
  local copies, waits for them, and re-layouts  0.61 us (2%)
    pallas_call x1, Pallas kernels, body(): pl.pallas_call(kernel, out_shape=pltpu.VMEM((32, 128), F32), in_specs=[pl...  35.1 us

profile of v6, /device:TPU:1, one launch (start us, length us, event | category | flops | bytes accessed | tf_op | source)
XLA Modules:
  0.0 35.7 jit_solution(5433391843346754327)
XLA Ops:
  0.0 35.1 %shard_map.64 = f32[32,128]{1,0:T(8,128)S(1)} custom-call(bf16[16,128,128]{2,1,0:T(8,128)(2,1)} %bitcast.9, s32[1,32]{1,0:T(1,128)} %bitcast.13, f32[2,4096]{1,0:T(2,128)} %matched_hbm.1, s32[2,2,1,14]{3,2,1,0:T(1,128)} %bitcast.10, f32[2,2,14]{2,1,0:T(2,128)} %bitcast.11, f32[2,14]{1,0:T(2,128)} %bitcast.12), custom_call_target="tpu_custom_call" | custom-call | tf_op jit(solution)/shard_map/pallas_call | solution.py:430
  35.1 0.6 %copy.9 = f32[32,128]{1,0:T(8,128)} copy(f32[32,128]{1,0:T(8,128)S(1)} %shard_map.64) | data formatting | bytes 32768
